TPU v7x, 32 devices: a whole 2x2x4 slice. The times are simulated.
32 devices in a mesh: rows: 8 (over z, y), rep: 4 (over x, core).
Axes of the slice: x: 2, y: 2, z: 4, core: 2. Of those that a mesh axis runs over, the one named last changes fastest.
Arguments:
- binned: int32 [8192, 1024], P('rows', 'rep'), may hold values from 0 to 127
- gradients: bfloat16 [8192], P('rows'), may hold values from -3 to 3
- hessians: bfloat16 [8192], P('rows'), may hold values from 0.019897461 to 0.25
- parents: int32 [8192], P('rows'), may hold values from 0 to 15
- split_feature: int32 [16], replicated, may hold values from 0 to 1023
- split_bin: int32 [16], replicated, may hold values from 32 to 95
- elected: int32 [32, 512], P(None, 'rep'), may hold values from 0 to 255
Outputs:
- new_nodes: int32 [8192], P('rows')
- best_gain: float32 [32, 4, 128], P(None, 'rep', 'rows')
- node_best: float32 [32], replicated
All inputs are finite; a program needn't handle non-finite values.
Results may differ from a plain program's by a relative error of at most 0.0003.
Values sent between devices are 32-bit elements; how exact they have to be, the bound alone decides.
A program may use at most 64 MiB of HBM per device.

v0:
```python
import functools

import jax
import jax.numpy as jnp
from jax import lax
from jax.experimental import pallas as pl
from jax.experimental.pallas import tpu as pltpu
from jax.sharding import PartitionSpec as P

BINS = 128
LANES = 128
MESH = pl.DeviceIdType.MESH

l2_penalty = 1.0


def kernel(
    n_rows, n_rep,
    split_feature_in, split_bin_in, binned_in, gradients_in, hessians_in, parents_in, elected_in,
    new_nodes, best_out, node_best,
    split_feature, split_bin, binned, gradients, hessians, parents, elected, in_sems, gh, left_bins, right_bins,
    side_snd, side_rcv, bins_snd, bins_rcv, node_rcv, gh_rcv, le, acc, top_snd, top_rcv,
    side_ss, side_rs, gh_ss, gh_rs, node_ss, node_rs, bins_ss, bins_rs, top_ss, top_rs,
):
    rows_here, block_width = binned.shape
    node_count, slots_here = elected.shape
    parent_count = split_feature.shape[0]
    owned = slots_here // n_rows
    me = lax.axis_index("rows")
    rep = lax.axis_index("rep")

    def partner(d):
        if n_rows & (n_rows - 1):
            return lax.rem(me + d, n_rows) if d else me
        other = me
        for bit in range(n_rows.bit_length()):
            if d >> bit & 1:
                other = other + (1 - 2 * lax.rem(me // 2**bit, 2)) * 2**bit
        return other

    def at_row(d):
        return (partner(d), rep)

    def at_rep(d):
        return (me, lax.rem(rep + d, n_rep))

    def send(src, dst, ss, rs, device):
        copy = pltpu.make_async_remote_copy(
            src_ref=src, dst_ref=dst, send_sem=ss, recv_sem=rs, device_id=device, device_id_type=MESH
        )
        copy.start()
        return copy

    barrier = pltpu.get_barrier_semaphore()
    others = [(d, e) for d in range(n_rows) for e in range(n_rep) if d or e]

    def at(d, e):
        return (partner(d), lax.rem(rep + e, n_rep))

    for d, e in others:
        pl.semaphore_signal(barrier, inc=1, device_id=at(d, e), device_id_type=MESH)

    loads = []
    for i, (src, dst) in enumerate(
        (
            (binned_in, binned), (split_feature_in, split_feature), (split_bin_in, split_bin), (parents_in, parents),
            (elected_in, elected), (gradients_in, gradients), (hessians_in, hessians),
        )
    ):
        loads.append(pltpu.make_async_copy(src, dst, in_sems.at[i]))
        loads[-1].start()
    for load in loads:
        load.wait()
    gh[0:1] = gradients[...].astype(jnp.float32).reshape(1, rows_here)
    gh[1:2] = hessians[...].astype(jnp.float32).reshape(1, rows_here)

    parent_sub = lax.broadcasted_iota(jnp.int32, (parent_count, block_width), 0)
    column = lax.broadcasted_iota(jnp.int32, (parent_count, block_width), 1) + rep * block_width
    feature_of = jnp.zeros((parent_count, block_width), jnp.int32)
    parent_row = lax.broadcasted_iota(jnp.int32, (parent_count, rows_here), 0)
    bin_of = jnp.zeros((parent_count, rows_here), jnp.int32)
    owns = jnp.zeros((parent_count, rows_here), jnp.int32)
    low = rep * block_width
    for p in range(parent_count):
        feature = split_feature[p]
        owned_here = jnp.where((feature >= low) & (feature < low + block_width), 1, 0)
        feature_of = jnp.where(parent_sub == p, feature, feature_of)
        bin_of = jnp.where(parent_row == p, split_bin[p], bin_of)
        owns = jnp.where(parent_row == p, owned_here, owns)
    picks = jnp.where(feature_of == column, 1.0, 0.0).astype(jnp.bfloat16)
    values = lax.dot_general(
        picks,
        binned[...].astype(jnp.float32).astype(jnp.bfloat16),
        (((1,), (1,)), ((), ())),
        preferred_element_type=jnp.float32,
    )
    own_parents = parents[...]
    goes = (parent_row == own_parents) & (owns > 0) & (values > bin_of.astype(jnp.float32))
    side = jnp.sum(jnp.where(goes, 1.0, 0.0), axis=0, keepdims=True)
    side_snd[...] = side

    node_sub = lax.broadcasted_iota(jnp.int32, (node_count, rows_here), 0)
    elected_wide = elected[...].astype(jnp.float32).astype(jnp.bfloat16)
    for child, turned in ((0, left_bins), (1, right_bins)):
        child_hot = jnp.where(node_sub == 2 * own_parents + child, 1.0, 0.0).astype(jnp.bfloat16)
        index = lax.dot_general(
            child_hot, elected_wide, (((0,), (0,)), ((), ())), preferred_element_type=jnp.float32
        ).astype(jnp.int32)
        lane = index % LANES
        part = index // LANES
        chosen = None
        for start in range(block_width // LANES):
            piece = binned[:, start * LANES : (start + 1) * LANES]
            found = jnp.take_along_axis(piece, lane, axis=1, mode="promise_in_bounds")
            chosen = found if chosen is None else jnp.where(part == start, found, chosen)
        turned[...] = chosen.astype(jnp.float32).T

    pl.semaphore_wait(barrier, len(others))
    copies = []
    for d in range(1, n_rep):
        copies.append(send(side_snd, side_rcv.at[d], side_ss.at[d], side_rs.at[d], at_rep(d)))
    for d in range(1, n_rows):
        copies.append(send(gh, gh_rcv.at[d], gh_ss.at[d], gh_rs.at[d], at_row(d)))
    gh_rcv[0] = gh[...]
    for d in range(1, n_rep):
        copies[d - 1].wait_recv()
        side = side + side_rcv[d]
    nodes = 2 * own_parents + side.astype(jnp.int32)
    new_nodes[...] = nodes
    node_rcv[0] = nodes

    for j in range(n_rows):
        slots = slice(j * owned, (j + 1) * owned)
        bins_snd[j] = jnp.where(side > 0.5, right_bins[slots, :], left_bins[slots, :])
    for d in range(1, n_rows):
        send(node_rcv.at[0], node_rcv.at[d], node_ss.at[d], node_rs.at[d], at_row(d))
        send(bins_snd.at[partner(d)], bins_rcv.at[d], bins_ss.at[d], bins_rs.at[d], at_row(d))
    bins_rcv[0] = bins_snd[me]

    def wait_for(d):
        for src, dst, ss, rs in (
            (gh, gh_rcv, gh_ss, gh_rs),
            (node_rcv.at[0], node_rcv, node_ss, node_rs),
            (bins_snd.at[0], bins_rcv, bins_ss, bins_rs),
        ):
            pltpu.make_async_remote_copy(
                src_ref=src, dst_ref=dst.at[d], send_sem=ss.at[d], recv_sem=rs.at[d],
                device_id=at_row(1), device_id_type=MESH,
            ).wait()

    bin_sub = lax.broadcasted_iota(jnp.int32, (BINS, rows_here), 0).astype(jnp.float32).astype(jnp.bfloat16)

    def add_source(d):
        there = node_sub == node_rcv[d]
        weights = jnp.concatenate(
            [jnp.where(there, gh_rcv[d, 0:1], 0.0), jnp.where(there, gh_rcv[d, 1:2], 0.0)], axis=0
        ).astype(jnp.bfloat16)
        bins = bins_rcv[d].astype(jnp.bfloat16)
        one = jnp.ones((), jnp.bfloat16)
        none = jnp.zeros((), jnp.bfloat16)
        for k in range(owned):
            le[k * BINS : (k + 1) * BINS, :] = jnp.where(bins[k : k + 1] <= bin_sub, one, none)
        return lax.dot_general(le[...], weights, (((1,), (1,)), ((), ())), preferred_element_type=jnp.float32)

    acc[...] = add_source(0)

    @pl.loop(1, n_rows)
    def _(d):
        wait_for(d)
        acc[...] += add_source(d)

    below = lax.broadcasted_iota(jnp.int32, (BINS, node_count), 0) < BINS - 1
    best = None
    for k in range(owned):
        left_grad = acc[k * BINS : (k + 1) * BINS, 0:node_count]
        left_hess = acc[k * BINS : (k + 1) * BINS, node_count : 2 * node_count]
        total_grad = left_grad[BINS - 1 : BINS]
        total_hess = left_hess[BINS - 1 : BINS]
        right_grad = total_grad - left_grad
        gain = 0.5 * (
            left_grad * left_grad / (left_hess + l2_penalty)
            + right_grad * right_grad / (total_hess - left_hess + l2_penalty)
            - total_grad * total_grad / (total_hess + l2_penalty)
        )
        top = jnp.max(jnp.where(below, gain, -jnp.inf), axis=0, keepdims=True)
        best_out[k : k + 1, :] = top
        best = top if best is None else jnp.maximum(best, top)

    top_snd[...] = best
    sent = []
    for i, (d, e) in enumerate(others):
        sent.append(send(top_snd, top_rcv.at[i], top_ss.at[i], top_rs.at[i], at(d, e)))
    for i, copy in enumerate(sent):
        copy.wait()
        best = jnp.maximum(best, top_rcv[i])
    node_best[...] = best
    for d in range(1, n_rep):
        copies[d - 1].wait_send()


def hand_on(*refs):
    for src, dst in zip(refs[:3], refs[3:]):
        dst[...] = src[...]


def body(n_rows, n_rep, binned, gradients, hessians, parents, split_feature, split_bin, elected):
    rows_here, block_width = binned.shape
    node_count, slots_here = elected.shape
    owned = slots_here // n_rows
    f32 = jnp.float32
    vmem = pl.BlockSpec(memory_space=pltpu.VMEM)
    dma = pltpu.SemaphoreType.DMA
    new_nodes, best, node_best = pl.pallas_call(
        functools.partial(kernel, n_rows, n_rep),
        out_shape=(
            jax.ShapeDtypeStruct((1, rows_here), jnp.int32),
            jax.ShapeDtypeStruct((owned, node_count), f32),
            jax.ShapeDtypeStruct((1, node_count), f32),
        ),
        in_specs=[pl.BlockSpec(memory_space=pl.ANY)] * 7,
        out_specs=(vmem, vmem, vmem),
        scratch_shapes=[
            pltpu.SMEM(split_feature.shape, jnp.int32),
            pltpu.SMEM(split_bin.shape, jnp.int32),
            pltpu.VMEM(binned.shape, jnp.int32),
            pltpu.VMEM(gradients.shape, gradients.dtype),
            pltpu.VMEM(hessians.shape, hessians.dtype),
            pltpu.VMEM((1, rows_here), jnp.int32),
            pltpu.VMEM(elected.shape, jnp.int32),
            dma((7,)),
            pltpu.VMEM((2, rows_here), f32),
            pltpu.VMEM((slots_here, rows_here), f32),
            pltpu.VMEM((slots_here, rows_here), f32),
            pltpu.VMEM((1, rows_here), f32),
            pltpu.VMEM((n_rep, 1, rows_here), f32),
            pltpu.VMEM((n_rows, owned, rows_here), f32),
            pltpu.VMEM((n_rows, owned, rows_here), f32),
            pltpu.VMEM((n_rows, 1, rows_here), jnp.int32),
            pltpu.VMEM((n_rows, 2, rows_here), f32),
            pltpu.VMEM((owned * BINS, rows_here), jnp.bfloat16),
            pltpu.VMEM((owned * BINS, 2 * node_count), f32),
            pltpu.VMEM((1, node_count), f32),
            pltpu.VMEM((n_rows * n_rep - 1, 1, node_count), f32),
        ]
        + [dma((n_rep,))] * 2 + [dma((n_rows,))] * 6 + [dma((n_rows * n_rep - 1,))] * 2,
        compiler_params=pltpu.CompilerParams(collective_id=0, has_side_effects=True),
    )(split_feature, split_bin, binned, gradients, hessians, parents.reshape(1, rows_here), elected)
    made = (new_nodes, best, node_best)
    new_nodes, best, node_best = pl.pallas_call(
        hand_on,
        out_shape=tuple(jax.ShapeDtypeStruct(a.shape, a.dtype) for a in made),
        in_specs=[vmem] * 3,
        out_specs=(vmem,) * 3,
    )(*made)
    return (
        new_nodes.reshape(rows_here),
        best.T.reshape(node_count, 1, owned),
        node_best.reshape(node_count),
    )


def solution(mesh):
    return jax.shard_map(
        functools.partial(body, mesh.shape["rows"], mesh.shape["rep"]),
        mesh=mesh,
        in_specs=(P("rows", "rep"), P("rows"), P("rows"), P("rows"), P(), P(), P(None, "rep")),
        out_specs=(P("rows"), P(None, "rep", "rows"), P()),
        check_vma=False,
    )
```

profile of v0, /device:TPU:0, one launch (start us, length us, event | category | flops | bytes accessed | tf_op | source)
XLA Modules:
  0.0 33.4 jit_solution(15617617142703734)
XLA Ops:
  0.6 31.4 %shard_map.94 = (s32[1,1024]{1,0:T(1,128)}, f32[16,32]{1,0:T(8,128)}, f32[1,32]{1,0:T(1,128)}) custom-call(s32[16]{0:T(128)} %split_feature_in.1, s32[16]{0:T(128)} %split_bin_in.1, s32[1024,256]{1,0:T(8,128)} %binned_in.1, bf16[1024]{0:T(1024)(128)(2,1)} %gradients_in.1, bf16[1024]{0:T(1024)(128)(2,1)} %hessians_in.1, s32[1,1024]{1,0:T(1,128)} %bitcast.6, ...), custom_call_target="tpu_custom_call" | custom-call | tf_op jit(solution)/shard_map/pallas_call | solution.py:213
  32.1 1.3 %shard_map.95 = (s32[1,1024]{1,0:T(1,128)}, f32[16,32]{1,0:T(8,128)}, f32[1,32]{1,0:T(1,128)}) custom-call(s32[1,1024]{1,0:T(1,128)} %get-tuple-element.9.refs_0_, f32[16,32]{1,0:T(8,128)} %get-tuple-element.10.refs_1_, f32[1,32]{1,0:T(1,128)} %get-tuple-element.11.refs_2_), custom_call_target="tpu_custom_call" | custom-call | tf_op jit(solution)/shard_map/pallas_call | solution.py:249
where the time goes:
time: 33.6 us; the launch traced here: 33.4 us
  Pallas kernels  32.7 us (97%)
  between operations  0.64 us (2%)
    pallas_call x1, Pallas kernels, body(): pl.pallas_call(functools.partial(kernel, n_rows, n_rep), out_shape=(jax.S...  31.4 us
    pallas_call x1, Pallas kernels, body(): pl.pallas_call(hand_on, out_shape=tuple((jax.ShapeDtypeStruct(a.shape, a....  1.3 us

commit v1 on v0

v1 whole, which is shorter than its diff:
```python
import functools

import jax
import jax.numpy as jnp
from jax import lax
from jax.experimental import pallas as pl
from jax.experimental.pallas import tpu as pltpu
from jax.sharding import PartitionSpec as P

BINS = 128
LANES = 128
MESH = pl.DeviceIdType.MESH

l2_penalty = 1.0


def partner_of(n_rows, me, d):
    if n_rows & (n_rows - 1):
        return lax.rem(me + d, n_rows) if d else me
    other = me
    for bit in range(n_rows.bit_length()):
        if d >> bit & 1:
            other = other + (1 - 2 * lax.rem(me // 2**bit, 2)) * 2**bit
    return other


def kernel(
    n_rows, n_rep, issue, arrive,
    split_feature_in, split_bin_in, binned_in, gradients_in, hessians_in, parents_in, elected_in,
    new_nodes, best_out, node_best,
    split_feature, split_bin, binned, gradients, hessians, parents, elected, in_sems, gh, left_bins, right_bins,
    side_snd, side_rcv, bins_snd, bins_rcv, node_rcv, gh_rcv, top_snd, top_rcv,
    side_ss, side_rs, gh_ss, gh_rs, node_ss, node_rs, bins_ss, bins_rs, top_ss, top_rs,
    le, acc,
):
    rows_here, block_width = binned.shape
    node_count, slots_here = elected.shape
    parent_count = split_feature.shape[0]
    owned = slots_here // n_rows
    me = lax.axis_index("rows")
    rep = lax.axis_index("rep")
    slot_of = {d: s for s, d in enumerate(arrive, 1)}

    def at(d, e):
        return (partner_of(n_rows, me, d), lax.rem(rep + e, n_rep))

    def send(src, dst, ss, rs, device):
        copy = pltpu.make_async_remote_copy(
            src_ref=src, dst_ref=dst, send_sem=ss, recv_sem=rs, device_id=device, device_id_type=MESH
        )
        copy.start()
        return copy

    with jax.named_scope("load"):
        barrier = pltpu.get_barrier_semaphore()
        greeted = [(0, e) for e in range(1, n_rep)] + [(d, 0) for d in issue]
        for d, e in greeted:
            pl.semaphore_signal(barrier, inc=1, device_id=at(d, e), device_id_type=MESH)

        loads = []
        for i, (src, dst) in enumerate(
            (
                (binned_in, binned), (split_feature_in, split_feature), (split_bin_in, split_bin), (parents_in, parents),
                (elected_in, elected), (gradients_in, gradients), (hessians_in, hessians),
            )
        ):
            loads.append(pltpu.make_async_copy(src, dst, in_sems.at[i]))
            loads[-1].start()
        for load in loads:
            load.wait()
        gh[0:1] = gradients[...].astype(jnp.float32).reshape(1, rows_here)
        gh[1:2] = hessians[...].astype(jnp.float32).reshape(1, rows_here)

    with jax.named_scope("side"):
        parent_sub = lax.broadcasted_iota(jnp.int32, (parent_count, block_width), 0)
        column = lax.broadcasted_iota(jnp.int32, (parent_count, block_width), 1) + rep * block_width
        feature_of = jnp.zeros((parent_count, block_width), jnp.int32)
        parent_row = lax.broadcasted_iota(jnp.int32, (parent_count, rows_here), 0)
        bin_of = jnp.zeros((parent_count, rows_here), jnp.int32)
        owns = jnp.zeros((parent_count, rows_here), jnp.int32)
        low = rep * block_width
        for p in range(parent_count):
            feature = split_feature[p]
            owned_here = jnp.where((feature >= low) & (feature < low + block_width), 1, 0)
            feature_of = jnp.where(parent_sub == p, feature, feature_of)
            bin_of = jnp.where(parent_row == p, split_bin[p], bin_of)
            owns = jnp.where(parent_row == p, owned_here, owns)
        picks = jnp.where(feature_of == column, 1.0, 0.0).astype(jnp.bfloat16)
        values = lax.dot_general(
            picks,
            binned[...].astype(jnp.float32).astype(jnp.bfloat16),
            (((1,), (1,)), ((), ())),
            preferred_element_type=jnp.float32,
        )
        own_parents = parents[...]
        goes = (parent_row == own_parents) & (owns > 0) & (values > bin_of.astype(jnp.float32))
        side = jnp.sum(jnp.where(goes, 1.0, 0.0), axis=0, keepdims=True)
        side_snd[...] = side

    with jax.named_scope("barwait"):
        pl.semaphore_wait(barrier, len(greeted))
        sides = []
        for e in range(1, n_rep):
            sides.append(send(side_snd, side_rcv.at[e], side_ss.at[e], side_rs.at[e], at(0, e)))
        ghs = []
        for d in issue:
            ghs.append(send(gh, gh_rcv.at[slot_of[d]], gh_ss.at[slot_of[d]], gh_rs.at[slot_of[d]], at(d, 0)))
        gh_rcv[0] = gh[...]

    with jax.named_scope("gather"):
        node_sub = lax.broadcasted_iota(jnp.int32, (node_count, rows_here), 0)
        elected_wide = elected[...].astype(jnp.float32).astype(jnp.bfloat16)
        for child, turned in ((0, left_bins), (1, right_bins)):
            child_hot = jnp.where(node_sub == 2 * own_parents + child, 1.0, 0.0).astype(jnp.bfloat16)
            index = lax.dot_general(
                child_hot, elected_wide, (((0,), (0,)), ((), ())), preferred_element_type=jnp.float32
            ).astype(jnp.int32)
            lane = index % LANES
            part = index // LANES
            chosen = None
            for start in range(block_width // LANES):
                piece = binned[:, start * LANES : (start + 1) * LANES]
                found = jnp.take_along_axis(piece, lane, axis=1, mode="promise_in_bounds")
                chosen = found if chosen is None else jnp.where(part == start, found, chosen)
            turned[...] = chosen.astype(jnp.float32).T

    with jax.named_scope("sidex"):
        for e, copy in enumerate(sides, 1):
            copy.wait()
            side = side + side_rcv[e]
        nodes = 2 * own_parents + side.astype(jnp.int32)
        new_nodes[...] = nodes
        node_rcv[0] = nodes

    with jax.named_scope("select"):
        for j in range(n_rows):
            slots = slice(j * owned, (j + 1) * owned)
            bins_snd[j] = jnp.where(side > 0.5, right_bins[slots, :], left_bins[slots, :])
        for d in issue:
            s = slot_of[d]
            send(node_rcv.at[0], node_rcv.at[s], node_ss.at[s], node_rs.at[s], at(d, 0))
            send(bins_snd.at[partner_of(n_rows, me, d)], bins_rcv.at[s], bins_ss.at[s], bins_rs.at[s], at(d, 0))
        bins_rcv[0] = bins_snd[me]

    def wait_for(s):
        for src, dst, ss, rs in (
            (gh, gh_rcv, gh_ss, gh_rs),
            (node_rcv.at[0], node_rcv, node_ss, node_rs),
            (bins_snd.at[0], bins_rcv, bins_ss, bins_rs),
        ):
            pltpu.make_async_remote_copy(
                src_ref=src, dst_ref=dst.at[s], send_sem=ss.at[s], recv_sem=rs.at[s],
                device_id=at(1, 0), device_id_type=MESH,
            ).wait()

    bin_sub = lax.broadcasted_iota(jnp.int32, (BINS, rows_here), 0).astype(jnp.float32).astype(jnp.bfloat16)
    one = jnp.ones((), jnp.bfloat16)
    none = jnp.zeros((), jnp.bfloat16)

    def add_source(s):
        there = node_sub == node_rcv[s]
        weights = jnp.concatenate(
            [jnp.where(there, gh_rcv[s, 0:1], 0.0), jnp.where(there, gh_rcv[s, 1:2], 0.0)], axis=0
        ).astype(jnp.bfloat16)
        bins = bins_rcv[s].astype(jnp.bfloat16)
        for k in range(owned):
            le[k * BINS : (k + 1) * BINS, :] = jnp.where(bins[k : k + 1] <= bin_sub, one, none).astype(le.dtype)
        return lax.dot_general(weights, le[...], (((1,), (1,)), ((), ())), preferred_element_type=jnp.float32)

    with jax.named_scope("src0"):
        acc[...] = add_source(0)

    with jax.named_scope("loop"):
        @pl.loop(1, n_rows)
        def _(s):
            with jax.named_scope("w"):
                wait_for(s)
            acc[...] += add_source(s)

    with jax.named_scope("gain"):
        lane = lax.broadcasted_iota(jnp.int32, (node_count, LANES), 1)
        total_grad = total_hess = base = None
        tops = jnp.full((node_count, LANES), -jnp.inf, jnp.float32)
        for k in range(owned):
                cols = slice(k * BINS, (k + 1) * BINS)
                left_grad = acc[0:node_count, cols]
                left_hess = acc[node_count : 2 * node_count, cols]
                if total_grad is None:
                    total_grad = jnp.broadcast_to(left_grad[:, BINS - 1 : BINS], left_grad.shape)
                    total_hess = jnp.broadcast_to(left_hess[:, BINS - 1 : BINS], left_hess.shape)
                    base = total_grad * total_grad / (total_hess + l2_penalty)
                right_grad = total_grad - left_grad
                gain = 0.5 * (
                    left_grad * left_grad / (left_hess + l2_penalty)
                    + right_grad * right_grad / (total_hess - left_hess + l2_penalty)
                    - base
                )
                top = jnp.max(jnp.where(lane < BINS - 1, gain, -jnp.inf), axis=1, keepdims=True)
                tops = jnp.where(lane == k, top, tops)
        turned = tops.T
        best_out[...] = turned[0:owned]
        best = jnp.max(turned[0:owned], axis=0, keepdims=True)
        top_snd[...] = best

    with jax.named_scope("top"):
        others = [(d, e) for d in (*issue, 0) for e in range(n_rep) if d or e]
        sent = []
        for i, (d, e) in enumerate(others):
            sent.append(send(top_snd, top_rcv.at[i], top_ss.at[i], top_rs.at[i], at(d, e)))
        for i, copy in enumerate(sent):
            copy.wait()
            best = jnp.maximum(best, top_rcv[i])
        node_best[...] = best


def hand_on(*refs):
    for src, dst in zip(refs[:3], refs[3:]):
        dst[...] = src[...]


def body(n_rows, n_rep, binned, gradients, hessians, parents, split_feature, split_bin, elected):
    rows_here, block_width = binned.shape
    node_count, slots_here = elected.shape
    owned = slots_here // n_rows
    f32 = jnp.float32
    vmem = pl.BlockSpec(memory_space=pltpu.VMEM)
    dma = pltpu.SemaphoreType.DMA
    order = tuple(range(1, n_rows))
    args = (split_feature, split_bin, binned, gradients, hessians, parents.reshape(1, rows_here), elected)
    made = pl.pallas_call(
        functools.partial(kernel, n_rows, n_rep, order, order),
        out_shape=(
            jax.ShapeDtypeStruct((1, rows_here), jnp.int32),
            jax.ShapeDtypeStruct((owned, node_count), f32),
            jax.ShapeDtypeStruct((1, node_count), f32),
        ),
        in_specs=[pl.BlockSpec(memory_space=pltpu.HBM)] * 7,
        out_specs=(vmem, vmem, vmem),
        scratch_shapes=[
            pltpu.SMEM(split_feature.shape, jnp.int32),
            pltpu.SMEM(split_bin.shape, jnp.int32),
            pltpu.VMEM(binned.shape, jnp.int32),
            pltpu.VMEM(gradients.shape, gradients.dtype),
            pltpu.VMEM(hessians.shape, hessians.dtype),
            pltpu.VMEM((1, rows_here), jnp.int32),
            pltpu.VMEM(elected.shape, jnp.int32),
            dma((7,)),
            pltpu.VMEM((2, rows_here), f32),
            pltpu.VMEM((slots_here, rows_here), f32),
            pltpu.VMEM((slots_here, rows_here), f32),
            pltpu.VMEM((1, rows_here), f32),
            pltpu.VMEM((n_rep, 1, rows_here), f32),
            pltpu.VMEM((n_rows, owned, rows_here), f32),
            pltpu.VMEM((n_rows, owned, rows_here), f32),
            pltpu.VMEM((n_rows, 1, rows_here), jnp.int32),
            pltpu.VMEM((n_rows, 2, rows_here), f32),
            pltpu.VMEM((1, node_count), f32),
            pltpu.VMEM((n_rows * n_rep - 1, 1, node_count), f32),
        ]
        + [dma((n_rep,))] * 2 + [dma((n_rows,))] * 6 + [dma((n_rows * n_rep - 1,))] * 2
        + [pltpu.VMEM((owned * BINS, rows_here), jnp.float8_e4m3fn), pltpu.VMEM((2 * node_count, owned * BINS), f32)],
        compiler_params=pltpu.CompilerParams(collective_id=0, has_side_effects=True, vmem_limit_bytes=16 * 2**20),
    )(*(pltpu.with_memory_space_constraint(a, pltpu.HBM) for a in args))
    new_nodes, best, node_best = pl.pallas_call(
        hand_on,
        out_shape=tuple(jax.ShapeDtypeStruct(a.shape, a.dtype) for a in made),
        in_specs=[vmem] * 3,
        out_specs=(vmem,) * 3,
        compiler_params=pltpu.CompilerParams(vmem_limit_bytes=2**20),
    )(*made)
    return (
        new_nodes.reshape(rows_here),
        best.T.reshape(node_count, 1, owned),
        node_best.reshape(node_count),
    )


def solution(mesh):
    return jax.shard_map(
        functools.partial(body, mesh.shape["rows"], mesh.shape["rep"]),
        mesh=mesh,
        in_specs=(P("rows", "rep"), P("rows"), P("rows"), P("rows"), P(), P(), P(None, "rep")),
        out_specs=(P("rows"), P(None, "rep", "rows"), P()),
        check_vma=False,
    )
```

time: 33.6 us -> 30.5 us (0.908)
  Pallas kernels: 32.7 us -> 29.7 us
    pallas_call x1, Pallas kernels: 31.4 us -> 29.1 us  [body(): pl.pallas_call(functools.partial(kernel, n_rows, n_rep, order, order), ou...]
    pallas_call x1, Pallas kernels: 1.3 us -> 0.6 us  [body(): pl.pallas_call(hand_on, out_shape=tuple((jax.ShapeDtypeStruct(a.shape, a....]
where the time goes in v1:
time: 30.5 us; the launch traced here: 30.3 us
  Pallas kernels  29.7 us (97%)
  between operations  0.64 us (2%)
    pallas_call x1, Pallas kernels, body(): pl.pallas_call(functools.partial(kernel, n_rows, n_rep, order, order), ou...  29.1 us

profile of v1, /device:TPU:0, one launch (start us, length us, event | category | flops | bytes accessed | tf_op | source)
XLA Modules:
  0.0 30.3 jit_solution(3396255495757661601)
XLA Ops:
  0.6 29.1 %shard_map.94 = (s32[1,1024]{1,0:T(1,128)S(1)}, f32[16,32]{1,0:T(8,128)S(1)}, f32[1,32]{1,0:T(1,128)S(1)}) custom-call(s32[16]{0:T(128)} %split_feature_in.1, s32[16]{0:T(128)} %split_bin_in.1, s32[1024,256]{1,0:T(8,128)} %binned_in.1, bf16[1024]{0:T(1024)(128)(2,1)} %gradients_in.1, bf16[1024]{0:T(1024)(128)(2,1)} %hessians_in.1, s32[1,1024]{1,0:T(1,128)} %bitcast.6, ...), custom_call_target="tpu_custom_call" | custom-call | tf_op jit(solution)/shard_map/pallas_call | solution.py:230
  29.7 0.6 %shard_map.95 = (s32[1,1024]{1,0:T(1,128)}, f32[16,32]{1,0:T(8,128)}, f32[1,32]{1,0:T(1,128)}) custom-call(s32[1,1024]{1,0:T(1,128)S(1)} %get-tuple-element.9.refs_0_, f32[16,32]{1,0:T(8,128)S(1)} %get-tuple-element.10.refs_1_, f32[1,32]{1,0:T(1,128)S(1)} %get-tuple-element.11.refs_2_), custom_call_target="tpu_custom_call" | custom-call | tf_op jit(solution)/shard_map/pallas_call | solution.py:264

commit v2 on v1

v2 whole, which is shorter than its diff:
```python
import functools

import jax
import jax.numpy as jnp
from jax import lax
from jax.experimental import pallas as pl
from jax.experimental.pallas import tpu as pltpu
from jax.sharding import PartitionSpec as P

BINS = 128
LANES = 128
MESH = pl.DeviceIdType.MESH

l2_penalty = 1.0


def partner_of(n_rows, me, d):
    if n_rows & (n_rows - 1):
        return lax.rem(me + d, n_rows) if d else me
    other = me
    for bit in range(n_rows.bit_length()):
        if d >> bit & 1:
            other = other + (1 - 2 * lax.rem(me // 2**bit, 2)) * 2**bit
    return other


def kernel(
    n_rows, n_rep, issue, arrive,
    split_feature_in, split_bin_in, binned_in, gradients_in, hessians_in, parents_in, elected_in,
    new_nodes, best_out, node_best,
    split_feature, split_bin, binned, gradients, hessians, parents, elected, both_bins,
    side_snd, side_rcv, bins_snd, bins_rcv, early, own_gh, weights, le, acc, top_snd, top_rcv,
    in_sems, side_ss, side_rs, early_ss, early_rs, fan_ss, fan_rs, bins_ss, bins_rs, top_ss, top_rs,
):
    rows_here, block_width = binned.shape
    node_count, slots_here = elected.shape
    parent_count = split_feature.shape[0]
    owned = slots_here // n_rows
    part_rows = rows_here // n_rep
    me = lax.axis_index("rows")
    rep = lax.axis_index("rep")
    slot_of = {d: s for s, d in enumerate(arrive, 1)}
    pieces = 2 if owned % 16 == 0 else 1
    share = owned // pieces

    def at(d, e):
        return (partner_of(n_rows, me, d), lax.rem(rep + e, n_rep))

    def remote(src, dst, ss, rs, device):
        return pltpu.make_async_remote_copy(
            src_ref=src, dst_ref=dst, send_sem=ss, recv_sem=rs, device_id=device, device_id_type=MESH
        )

    def all_of(ref, ss, rs):
        return remote(ref, ref, ss, rs, at(1, 0))

    with jax.named_scope("load"):
        barrier = pltpu.get_barrier_semaphore()
        greeted = [(0, e) for e in range(1, n_rep)] + [(d, 0) for d in issue]
        for d, e in greeted:
            pl.semaphore_signal(barrier, inc=1, device_id=at(d, e), device_id_type=MESH)

        loads = []
        quarter = rows_here // 4
        for i, (src, dst) in enumerate(
            (
                (split_feature_in, split_feature), (split_bin_in, split_bin), (parents_in, parents),
                *((binned_in.at[c * quarter : (c + 1) * quarter], binned.at[c * quarter : (c + 1) * quarter]) for c in range(4)),
                (gradients_in, gradients), (hessians_in, hessians), (elected_in, elected),
            )
        ):
            loads.append(pltpu.make_async_copy(src, dst, in_sems.at[i]))
            loads[-1].start()
        for load in loads[:3]:
            load.wait()

    with jax.named_scope("side"):
        parent_sub = lax.broadcasted_iota(jnp.int32, (parent_count, block_width), 0)
        column = lax.broadcasted_iota(jnp.int32, (parent_count, block_width), 1) + rep * block_width
        feature_of = jnp.zeros((parent_count, block_width), jnp.int32)
        parent_row = lax.broadcasted_iota(jnp.int32, (parent_count, rows_here), 0)
        bin_of = jnp.zeros((parent_count, rows_here), jnp.int32)
        owns = jnp.zeros((parent_count, rows_here), jnp.int32)
        low = rep * block_width
        for p in range(parent_count):
            feature = split_feature[p]
            owned_here = jnp.where((feature >= low) & (feature < low + block_width), 1, 0)
            feature_of = jnp.where(parent_sub == p, feature, feature_of)
            bin_of = jnp.where(parent_row == p, split_bin[p], bin_of)
            owns = jnp.where(parent_row == p, owned_here, owns)
        for load in loads[3:7]:
            load.wait()
        picks = jnp.where(feature_of == column, 1.0, 0.0).astype(jnp.bfloat16)
        values = lax.dot_general(
            picks,
            binned[...].astype(jnp.float32).astype(jnp.bfloat16),
            (((1,), (1,)), ((), ())),
            preferred_element_type=jnp.float32,
        )
        own_parents = parents[...]
        goes = (parent_row == own_parents) & (owns > 0) & (values > bin_of.astype(jnp.float32))
        side = jnp.sum(jnp.where(goes, 1.0, 0.0), axis=0, keepdims=True)
        side_snd[...] = side
        for load in loads[7:9]:
            load.wait()
        own_gh[0:1] = gradients[...].astype(jnp.float32).reshape(1, rows_here)
        own_gh[1:2] = hessians[...].astype(jnp.float32).reshape(1, rows_here)
        mine = pl.ds(pl.multiple_of(rep * part_rows, part_rows), part_rows)
        for f in range(n_rep):
            early[0, 0, f : f + 1] = side[:, f * part_rows : (f + 1) * part_rows]
        early[0, 0, n_rep : n_rep + 2] = own_gh[:, mine]
        early[0, 0, n_rep + 2 : n_rep + 3] = parents[:, mine].astype(jnp.float32)
        early[0, 0, n_rep + 3 :] = jnp.zeros((early.shape[2] - n_rep - 3, part_rows), jnp.float32)

    with jax.named_scope("barwait"):
        pl.semaphore_wait(barrier, len(greeted))
        for e in range(1, n_rep):
            remote(side_snd, side_rcv.at[e - 1], side_ss, side_rs, at(0, e)).start()
        for d in issue:
            remote(early.at[0, 0], early.at[0, slot_of[d]], early_ss, early_rs, at(d, 0)).start()

    with jax.named_scope("gather"):
        loads[9].wait()
        elected_wide = elected[...].astype(jnp.float32).astype(jnp.bfloat16)
        tile = rows_here // 2
        node_tile = lax.broadcasted_iota(jnp.int32, (node_count, tile), 0)

        @pl.loop(0, rows_here // tile)
        def _(t):
            here = pl.ds(pl.multiple_of(t * tile, tile), tile)
            above = 2 * parents[:, here]
            packed = None
            for child in range(2):
                child_hot = jnp.where(node_tile == above + child, 1.0, 0.0).astype(jnp.bfloat16)
                index = lax.dot_general(
                    child_hot, elected_wide, (((0,), (0,)), ((), ())), preferred_element_type=jnp.float32
                ).astype(jnp.int32)
                lane = index & (LANES - 1)
                part = lax.shift_right_logical(index, LANES.bit_length() - 1)
                chosen = None
                for start in range(block_width // LANES):
                    piece = binned[here, start * LANES : (start + 1) * LANES]
                    found = jnp.take_along_axis(piece, lane, axis=1, mode="promise_in_bounds")
                    chosen = found if chosen is None else jnp.where(part == start, found, chosen)
                packed = chosen if packed is None else packed + chosen * 256
            both_bins[:, here] = packed.T

    with jax.named_scope("sidex"):
        sides = all_of(side_rcv, side_ss, side_rs)
        sides.wait_recv()
        for e in range(1, n_rep):
            side = side + side_rcv[e - 1]
        side = side.astype(jnp.int32)
        nodes = 2 * parents[...] + side
        new_nodes[...] = nodes

    with jax.named_scope("select"):
        shift = side * 8
        for j in range(n_rows):
            slots = slice(j * owned, (j + 1) * owned)
            bins_snd[j] = lax.shift_right_logical(both_bins[slots, :], jnp.broadcast_to(shift, (owned, rows_here))) & 255
        for d in issue:
            s = slot_of[d]
            for piece in range(pieces):
                some = slice(piece * share, (piece + 1) * share)
                remote(
                    bins_snd.at[partner_of(n_rows, me, d), some], bins_rcv.at[s, some],
                    bins_ss, bins_rs.at[s * pieces + piece], at(d, 0),
                ).start()
        bins_rcv[0] = bins_snd[me]

    with jax.named_scope("nodew"):
        earlies = all_of(early.at[0, 1:n_rows], early_ss, early_rs)
        earlies.wait_recv()
        for e in range(1, n_rep):
            remote(early.at[0, 1:n_rows], early.at[e, 1:n_rows], fan_ss, fan_rs, at(0, e)).start()
        fans = all_of(early.at[1:n_rep, 1:n_rows], fan_ss, fan_rs)

    bin_sub = lax.broadcasted_iota(jnp.int32, (BINS, rows_here), 0).astype(jnp.float32).astype(jnp.bfloat16)
    node_sub = lax.broadcasted_iota(jnp.int32, (node_count, rows_here), 0)
    one = jnp.ones((), jnp.bfloat16)
    none = jnp.zeros((), jnp.bfloat16)
    acc[...] = jnp.zeros_like(acc)

    def weigh(node, grad, hess):
        there = node_sub == node
        return jnp.concatenate([jnp.where(there, grad, 0.0), jnp.where(there, hess, 0.0)], axis=0).astype(jnp.bfloat16)

    weights[0] = weigh(nodes, own_gh[0:1], own_gh[1:2])

    with jax.named_scope("loop"):
        @pl.loop(0, n_rows * pieces)
        def _(t):
            s = t // pieces
            piece = t % pieces
            first = pl.multiple_of(piece * share, share)
            with jax.named_scope("w"):
                @pl.when(t == pieces)
                def _():
                    fans.wait_recv()

                    @pl.loop(1, n_rows)
                    def _(u):
                        node, grad, hess = [], [], []
                        for f in range(n_rep):
                            e = lax.rem(rep + n_rep - f, n_rep)
                            node.append(
                                2.0 * early[e, u, n_rep + 2 : n_rep + 3]
                                + sum(early[c, u, f : f + 1] for c in range(n_rep))
                            )
                            grad.append(early[e, u, n_rep : n_rep + 1])
                            hess.append(early[e, u, n_rep + 1 : n_rep + 2])
                        node, grad, hess = (jnp.concatenate(x, axis=1) for x in (node, grad, hess))
                        weights[u] = weigh(node.astype(jnp.int32), grad, hess)

                @pl.when(s > 0)
                def _():
                    all_of(bins_rcv.at[s, pl.ds(first, share)], bins_ss, bins_rs.at[t]).wait_recv()
            bins = bins_rcv[s, pl.ds(first, share), :].astype(jnp.float32).astype(jnp.bfloat16)
            for k in range(share):
                le[k * BINS : (k + 1) * BINS, :] = jnp.where(bins[k : k + 1] <= bin_sub, one, none).astype(le.dtype)
            acc[piece] += lax.dot_general(
                weights[s], le[...], (((1,), (1,)), ((), ())), preferred_element_type=jnp.float32
            )

    with jax.named_scope("gain"):
        lane = lax.broadcasted_iota(jnp.int32, (node_count, LANES), 1)
        total_grad = total_hess = base = None
        tops = jnp.full((node_count, LANES), -jnp.inf, jnp.float32)
        for k in range(owned):
                cols = slice(k % share * BINS, (k % share + 1) * BINS)
                left_grad = acc[k // share, 0:node_count, cols]
                left_hess = acc[k // share, node_count : 2 * node_count, cols]
                if total_grad is None:
                    total_grad = jnp.broadcast_to(left_grad[:, BINS - 1 : BINS], left_grad.shape)
                    total_hess = jnp.broadcast_to(left_hess[:, BINS - 1 : BINS], left_hess.shape)
                    base = total_grad * total_grad / (total_hess + l2_penalty)
                right_grad = total_grad - left_grad
                gain = 0.5 * (
                    left_grad * left_grad / (left_hess + l2_penalty)
                    + right_grad * right_grad / (total_hess - left_hess + l2_penalty)
                    - base
                )
                top = jnp.max(jnp.where(lane < BINS - 1, gain, -jnp.inf), axis=1, keepdims=True)
                tops = jnp.where(lane == k, top, tops)
        turned = tops.T
        best_out[...] = turned[0:owned]
        best = jnp.max(turned[0:owned], axis=0, keepdims=True)
        top_snd[...] = best

    with jax.named_scope("top"):
        others = [(d, e) for d in (*issue, 0) for e in range(n_rep) if d or e]
        for i, (d, e) in enumerate(others):
            remote(top_snd, top_rcv.at[i], top_ss, top_rs, at(d, e)).start()
        tops_all = all_of(top_rcv, top_ss, top_rs)
        tops_all.wait_recv()
        for i in range(len(others)):
            best = jnp.maximum(best, top_rcv[i])
        node_best[...] = best
        for sent in (sides, earlies, fans, all_of(bins_rcv.at[1:n_rows], bins_ss, bins_rs.at[0]), tops_all):
            sent.wait_send()


def hand_on(*refs):
    for src, dst in zip(refs[:3], refs[3:]):
        dst[...] = src[...]


def body(n_rows, n_rep, binned, gradients, hessians, parents, split_feature, split_bin, elected):
    rows_here, block_width = binned.shape
    node_count, slots_here = elected.shape
    owned = slots_here // n_rows
    pieces = 2 if owned % 16 == 0 else 1
    f32 = jnp.float32
    vmem = pl.BlockSpec(memory_space=pltpu.VMEM)
    dma = pltpu.SemaphoreType.DMA
    order = tuple(range(1, n_rows))
    args = (split_feature, split_bin, binned, gradients, hessians, parents.reshape(1, rows_here), elected)
    made = pl.pallas_call(
        functools.partial(kernel, n_rows, n_rep, order, order),
        out_shape=(
            jax.ShapeDtypeStruct((1, rows_here), jnp.int32),
            jax.ShapeDtypeStruct((owned, node_count), f32),
            jax.ShapeDtypeStruct((1, node_count), f32),
        ),
        in_specs=[pl.BlockSpec(memory_space=pltpu.HBM)] * 7,
        out_specs=(vmem, vmem, vmem),
        scratch_shapes=[
            pltpu.SMEM(split_feature.shape, jnp.int32),
            pltpu.SMEM(split_bin.shape, jnp.int32),
            pltpu.VMEM(binned.shape, jnp.int32),
            pltpu.VMEM(gradients.shape, gradients.dtype),
            pltpu.VMEM(hessians.shape, hessians.dtype),
            pltpu.VMEM((1, rows_here), jnp.int32),
            pltpu.VMEM(elected.shape, jnp.int32),
            pltpu.VMEM((slots_here, rows_here), jnp.int32),
            pltpu.VMEM((1, rows_here), f32),
            pltpu.VMEM((n_rep - 1, 1, rows_here), f32),
            pltpu.VMEM((n_rows, owned, rows_here), jnp.int32),
            pltpu.VMEM((n_rows, owned, rows_here), jnp.int32),
            pltpu.VMEM((n_rep, n_rows, -(-(n_rep + 3) // 8) * 8, rows_here // n_rep), f32),
            pltpu.VMEM((2, rows_here), f32),
            pltpu.VMEM((n_rows, 2 * node_count, rows_here), jnp.bfloat16),
            pltpu.VMEM((owned // pieces * BINS, rows_here), jnp.float8_e4m3fn),
            pltpu.VMEM((pieces, 2 * node_count, owned // pieces * BINS), f32),
            pltpu.VMEM((1, node_count), f32),
            pltpu.VMEM((n_rows * n_rep - 1, 1, node_count), f32),
            dma((10,)),
        ]
        + [dma(())] * 7
        + [dma((n_rows * pieces,))]
        + [dma(())] * 2,
        compiler_params=pltpu.CompilerParams(collective_id=0, has_side_effects=True, vmem_limit_bytes=16 * 2**20),
    )(*(pltpu.with_memory_space_constraint(a, pltpu.HBM) for a in args))
    new_nodes, best, node_best = pl.pallas_call(
        hand_on,
        out_shape=tuple(jax.ShapeDtypeStruct(a.shape, a.dtype) for a in made),
        in_specs=[vmem] * 3,
        out_specs=(vmem,) * 3,
        compiler_params=pltpu.CompilerParams(vmem_limit_bytes=2**20),
    )(*made)
    return (
        new_nodes.reshape(rows_here),
        best.T.reshape(node_count, 1, owned),
        node_best.reshape(node_count),
    )


def solution(mesh):
    return jax.shard_map(
        functools.partial(body, mesh.shape["rows"], mesh.shape["rep"]),
        mesh=mesh,
        in_specs=(P("rows", "rep"), P("rows"), P("rows"), P("rows"), P(), P(), P(None, "rep")),
        out_specs=(P("rows"), P(None, "rep", "rows"), P()),
        check_vma=False,
    )
```

time: 30.5 us -> 28.7 us (0.941)
  Pallas kernels: 29.7 us -> 27.9 us
    pallas_call x1, Pallas kernels: 29.1 us -> 27.3 us  [body(): pl.pallas_call(functools.partial(kernel, n_rows, n_rep, order, order), ou...]
where the time goes in v2:
time: 28.7 us; the launch traced here: 28.6 us
  Pallas kernels  27.9 us (97%)
  between operations  0.64 us (2%)
    pallas_call x1, Pallas kernels, body(): pl.pallas_call(functools.partial(kernel, n_rows, n_rep, order, order), ou...  27.3 us
    pallas_call x1, Pallas kernels, body(): pl.pallas_call(hand_on, out_shape=tuple((jax.ShapeDtypeStruct(a.shape, a....  0.6 us

profile of v2, /device:TPU:0, one launch (start us, length us, event | category | flops | bytes accessed | tf_op | source)
XLA Modules:
  0.0 28.6 jit_solution(4860798675901108979)
XLA Ops:
  0.6 27.3 %shard_map.94 = (s32[1,1024]{1,0:T(1,128)S(1)}, f32[16,32]{1,0:T(8,128)S(1)}, f32[1,32]{1,0:T(1,128)S(1)}) custom-call(s32[16]{0:T(128)} %split_feature_in.1, s32[16]{0:T(128)} %split_bin_in.1, s32[1024,256]{1,0:T(8,128)} %binned_in.1, bf16[1024]{0:T(1024)(128)(2,1)} %gradients_in.1, bf16[1024]{0:T(1024)(128)(2,1)} %hessians_in.1, s32[1,1024]{1,0:T(1,128)} %bitcast.6, ...), custom_call_target="tpu_custom_call" | custom-call | tf_op jit(solution)/shard_map/pallas_call | solution.py:279
  28.0 0.6 %shard_map.95 = (s32[1,1024]{1,0:T(1,128)}, f32[16,32]{1,0:T(8,128)}, f32[1,32]{1,0:T(1,128)}) custom-call(s32[1,1024]{1,0:T(1,128)S(1)} %get-tuple-element.9.refs_0_, f32[16,32]{1,0:T(8,128)S(1)} %get-tuple-element.10.refs_1_, f32[1,32]{1,0:T(1,128)S(1)} %get-tuple-element.11.refs_2_), custom_call_target="tpu_custom_call" | custom-call | tf_op jit(solution)/shard_map/pallas_call | solution.py:315

commit v3 on v2

v3 whole, which is shorter than its diff:
```python
import functools

import jax
import jax.numpy as jnp
from jax import lax
from jax.experimental import pallas as pl
from jax.experimental.pallas import tpu as pltpu
from jax.sharding import PartitionSpec as P

BINS = 128
LANES = 128
MESH = pl.DeviceIdType.MESH

l2_penalty = 1.0


def partner_of(n_rows, me, d):
    if n_rows & (n_rows - 1):
        return lax.rem(me + d, n_rows) if d else me
    other = me
    for bit in range(n_rows.bit_length()):
        if d >> bit & 1:
            other = other + (1 - 2 * lax.rem(me // 2**bit, 2)) * 2**bit
    return other


def parts_of(pieces, owned, rows_here):
    everything = slice(0, owned), slice(0, rows_here)
    if pieces == 1:
        return [everything], [[everything]]
    share = owned // pieces
    step = max(rows_here // 4, 2 * LANES)
    upper, lower = slice(0, share), slice(share, owned)
    usual = [(upper, slice(0, rows_here)), (lower, slice(LANES, rows_here))]
    last = [[(upper, slice(0, step)), (lower, slice(LANES, step))]]
    for begin in range(step, rows_here, step):
        last.append([(slice(0, owned), slice(begin, min(begin + step, rows_here)))])
    return usual, last


def kernel(
    n_rows, n_rep, pieces, issue, arrive,
    split_feature_in, split_bin_in, binned_in, gradients_in, hessians_in, parents_in, elected_in,
    new_nodes, best_out, node_best,
    split_feature, split_bin, binned, gradients, hessians, parents, elected, both_bins,
    side_snd, side_rcv, guess_snd, guess_rcv, bins_snd, bins_rcv, early, own_gh, weights, le, acc, top_snd, top_rcv,
    in_sems, side_ss, side_rs, early_ss, early_rs, fan_ss, fan_rs, guess_ss, guess_rs, bins_ss, bins_rs, top_ss, top_rs,
):
    rows_here, block_width = binned.shape
    node_count, slots_here = elected.shape
    parent_count = split_feature.shape[0]
    owned = slots_here // n_rows
    part_rows = rows_here // n_rep
    me = lax.axis_index("rows")
    rep = lax.axis_index("rep")
    slot_of = {d: s for s, d in enumerate(arrive, 1)}
    share = owned // pieces
    parts, steps = parts_of(pieces, owned, rows_here)
    ends = [part for step in steps for part in step]
    hedged = slice(owned - share, owned)
    groups = [(1, n_rows)]

    def at(d, e):
        return (partner_of(n_rows, me, d), lax.rem(rep + e, n_rep))

    def remote(src, dst, ss, rs, device):
        return pltpu.make_async_remote_copy(
            src_ref=src, dst_ref=dst, send_sem=ss, recv_sem=rs, device_id=device, device_id_type=MESH
        )

    def all_of(ref, ss, rs):
        return remote(ref, ref, ss, rs, at(1, 0))

    with jax.named_scope("load"):
        barrier = pltpu.get_barrier_semaphore()
        greeted = [(0, e) for e in range(1, n_rep)] + [(d, 0) for d in issue]
        for d, e in greeted:
            pl.semaphore_signal(barrier, inc=1, device_id=at(d, e), device_id_type=MESH)

        loads = []
        for i, (src, dst) in enumerate(
            (
                (split_feature_in, split_feature), (split_bin_in, split_bin), (parents_in, parents),
                (binned_in, binned),
                (gradients_in, gradients), (hessians_in, hessians), (elected_in, elected),
            )
        ):
            loads.append(pltpu.make_async_copy(src, dst, in_sems.at[i]))
            loads[-1].start()
        for load in loads[:3]:
            load.wait()

    with jax.named_scope("side"):
        parent_sub = lax.broadcasted_iota(jnp.int32, (parent_count, block_width), 0)
        column = lax.broadcasted_iota(jnp.int32, (parent_count, block_width), 1) + rep * block_width
        feature_of = jnp.zeros((parent_count, block_width), jnp.int32)
        parent_row = lax.broadcasted_iota(jnp.int32, (parent_count, rows_here), 0)
        bin_of = jnp.zeros((parent_count, rows_here), jnp.int32)
        owns = jnp.zeros((parent_count, rows_here), jnp.int32)
        low = rep * block_width
        for p in range(parent_count):
            feature = split_feature[p]
            owned_here = jnp.where((feature >= low) & (feature < low + block_width), 1, 0)
            feature_of = jnp.where(parent_sub == p, feature, feature_of)
            bin_of = jnp.where(parent_row == p, split_bin[p], bin_of)
            owns = jnp.where(parent_row == p, owned_here, owns)
        for load in loads[3:4]:
            load.wait()
        picks = jnp.where(feature_of == column, 1.0, 0.0).astype(jnp.bfloat16)
        values = lax.dot_general(
            picks,
            binned[...].astype(jnp.float32).astype(jnp.bfloat16),
            (((1,), (1,)), ((), ())),
            preferred_element_type=jnp.float32,
        )
        own_parents = parents[...]
        goes = (parent_row == own_parents) & (owns > 0) & (values > bin_of.astype(jnp.float32))
        side = jnp.sum(jnp.where(goes, 1.0, 0.0), axis=0, keepdims=True)
        side_snd[...] = side
        for load in loads[4:6]:
            load.wait()
        own_gh[0:1] = gradients[...].astype(jnp.float32).reshape(1, rows_here)
        own_gh[1:2] = hessians[...].astype(jnp.float32).reshape(1, rows_here)
        mine = pl.ds(pl.multiple_of(rep * part_rows, part_rows), part_rows)
        for f in range(n_rep):
            early[0, 0, f] = side[:, f * part_rows : (f + 1) * part_rows]
        early[0, 0, n_rep] = own_gh[0:1, mine]
        early[0, 0, n_rep + 1] = own_gh[1:2, mine]
        early[0, 0, n_rep + 2] = parents[:, mine].astype(jnp.float32)

    with jax.named_scope("barwait"):
        pl.semaphore_wait(barrier, len(greeted))
        for e in range(1, n_rep):
            remote(side_snd, side_rcv.at[e - 1], side_ss, side_rs, at(0, e)).start()
        for d in issue[::-1]:
            s = slot_of[d]
            g = [i for i, (low, high) in enumerate(groups) if low <= s < high][0]
            remote(early.at[0, 0], early.at[0, s], early_ss.at[g], early_rs.at[g], at(d, 0)).start()

    with jax.named_scope("gather"):
        loads[6].wait()
        elected_wide = elected[...].astype(jnp.float32).astype(jnp.bfloat16)

        def gather(begin, end):
            here = slice(begin, end)
            node_tile = lax.broadcasted_iota(jnp.int32, (node_count, end - begin), 0)
            above = 2 * own_parents[:, here]
            pieces_here = [
                binned[here, start * LANES : (start + 1) * LANES] for start in range(block_width // LANES)
            ]
            tables = [
                pieces_here[g] + (pieces_here[g + 1] * 256 if g + 1 < len(pieces_here) else 0)
                for g in range(0, len(pieces_here), 2)
            ]
            packed = None
            for child in range(2):
                child_hot = jnp.where(node_tile == above + child, 1.0, 0.0).astype(jnp.bfloat16)
                index = lax.dot_general(
                    child_hot, elected_wide, (((0,), (0,)), ((), ())), preferred_element_type=jnp.float32
                ).astype(jnp.int32)
                lane = index & (LANES - 1)
                part = lax.shift_right_logical(index, LANES.bit_length() - 1)
                chosen = None
                for g, table in enumerate(tables):
                    found = jnp.take_along_axis(table, lane, axis=1, mode="promise_in_bounds")
                    found = lax.shift_right_logical(found, (part & 1) * 8) & 255
                    chosen = found if chosen is None else jnp.where(part // 2 == g, found, chosen)
                packed = chosen if packed is None else packed + chosen * 256
            both_bins[:, here] = packed.T

        gather(0, LANES)
        if pieces > 1:
            for j in range(n_rows):
                two = both_bins[j * owned + owned - share : (j + 1) * owned, 0:LANES]
                guess_snd[j, 0] = two & 255
                guess_snd[j, 1] = lax.shift_right_logical(two, 8)
            for d in issue:
                remote(
                    guess_snd.at[partner_of(n_rows, me, d)], guess_rcv.at[slot_of[d]], guess_ss, guess_rs, at(d, 0)
                ).start()
        gather(LANES, rows_here)

    with jax.named_scope("sidex"):
        sides = all_of(side_rcv, side_ss, side_rs)
        sides.wait_recv()
        for e in range(1, n_rep):
            side = side + side_rcv[e - 1]
        side = side.astype(jnp.int32)
        nodes = 2 * parents[...] + side
        new_nodes[...] = nodes

    with jax.named_scope("select"):
        shift = side * 8
        for j in range(n_rows):
            slots = slice(j * owned, (j + 1) * owned)
            bins_snd[j] = lax.shift_right_logical(both_bins[slots, :], jnp.broadcast_to(shift, (owned, rows_here))) & 255
        for d in issue:
            s = slot_of[d]
            for i, (slots, rows) in enumerate(ends if s == n_rows - 1 else parts):
                remote(
                    bins_snd.at[partner_of(n_rows, me, d), slots, rows], bins_rcv.at[s, slots, rows],
                    bins_ss.at[i + (len(parts) if s == n_rows - 1 else 0)], bins_rs.at[(s - 1) * len(parts) + i], at(d, 0),
                ).start()
        bins_rcv[0] = bins_snd[me]

    def early_of(g):
        return all_of(early.at[0, groups[g][0] : groups[g][1]], early_ss.at[g], early_rs.at[g])

    def fan_of(g):
        return all_of(early.at[1:n_rep, groups[g][0] : groups[g][1]], fan_ss.at[g], fan_rs.at[g])

    def fan(g):
        early_of(g).wait_recv()
        some = slice(*groups[g])
        for e in range(1, n_rep):
            remote(early.at[0, some], early.at[e, some], fan_ss.at[g], fan_rs.at[g], at(0, e)).start()

    with jax.named_scope("nodew"):
        fan(0)

    bin_sub = lax.broadcasted_iota(jnp.int32, (BINS, rows_here), 0).astype(jnp.float32).astype(jnp.bfloat16)
    node_sub = lax.broadcasted_iota(jnp.int32, (node_count, rows_here), 0)
    one = jnp.ones((), jnp.bfloat16)
    none = jnp.zeros((), jnp.bfloat16)
    acc[...] = jnp.zeros_like(acc)

    def weigh(node, grad, hess):
        there = node_sub == node
        return jnp.concatenate([jnp.where(there, grad, 0.0), jnp.where(there, hess, 0.0)], axis=0).astype(jnp.bfloat16)

    weights[0] = weigh(nodes, own_gh[0:1], own_gh[1:2])

    def arrived(s, i):
        slots, rows = parts[i]
        all_of(bins_rcv.at[s, slots, rows], bins_ss.at[i], bins_rs.at[(s - 1) * len(parts) + i]).wait_recv()

    def ended(i):
        slots, rows = ends[i]
        return all_of(
            bins_rcv.at[n_rows - 1, slots, rows], bins_ss.at[len(parts) + i], bins_rs.at[(n_rows - 2) * len(parts) + i]
        )

    def add(s, slots, rows):
        bins = bins_rcv[s, slots, rows].astype(jnp.float32).astype(jnp.bfloat16)
        cols = slice(slots.start * BINS, slots.stop * BINS)
        for k in range(slots.stop - slots.start):
            at_k = slice((slots.start + k) * BINS, (slots.start + k + 1) * BINS)
            le[at_k, rows] = jnp.where(bins[k : k + 1] <= bin_sub[:, rows], one, none).astype(le.dtype)
        acc[:, cols] += lax.dot_general(
            weights[s, :, rows], le[cols, rows], (((1,), (1,)), ((), ())), preferred_element_type=jnp.float32
        )

    guesses = all_of(guess_rcv.at[1:n_rows], guess_ss, guess_rs) if pieces > 1 else None

    def fill(g):
        fan_of(g).wait_recv()

        @pl.loop(*groups[g])
        def _(u):
            above, right, grad, hess = [], [], [], []
            for f in range(n_rep):
                e = lax.rem(rep + n_rep - f, n_rep)
                above.append(early[e, u, n_rep + 2])
                right.append(sum(early[c, u, f] for c in range(n_rep)))
                grad.append(early[e, u, n_rep])
                hess.append(early[e, u, n_rep + 1])
            above, right, grad, hess = (jnp.concatenate(x, axis=1) for x in (above, right, grad, hess))
            weights[u] = weigh((2.0 * above + right).astype(jnp.int32), grad, hess)
            if pieces > 1:
                bins_rcv[u, hedged, 0:LANES] = jnp.where(right[:, 0:LANES] > 0.5, guess_rcv[u, 1], guess_rcv[u, 0])

    everything = slice(0, rows_here)
    with jax.named_scope("own"):
        for piece in range(pieces):
            add(0, slice(piece * share, (piece + 1) * share), everything)
        for g in range(1, len(groups)):
            fan(g)
        if pieces > 1:
            guesses.wait_recv()
    with jax.named_scope("fill"):
        fill(0)

    with jax.named_scope("loop"):
        @pl.loop(1, n_rows - 1)
        def _(s):
            for piece in range(pieces):
                with jax.named_scope("w"):
                    arrived(s, piece)
                add(s, slice(piece * share, (piece + 1) * share), everything)

    i = 0
    for step in steps:
        with jax.named_scope("last"):
            with jax.named_scope("lw"):
                for _ in step:
                    ended(i).wait_recv()
                    i += 1
            add(n_rows - 1, slice(0, owned), slice(0 if step is steps[0] else step[0][1].start, step[0][1].stop))

    lane = lax.broadcasted_iota(jnp.int32, (node_count, LANES), 1)
    tops = jnp.full((node_count, LANES), -jnp.inf, jnp.float32)
    total_grad = total_hess = base = None
    for piece in range(pieces):
        with jax.named_scope("gain"):
            for k in range(share):
                cols = slice((piece * share + k) * BINS, (piece * share + k + 1) * BINS)
                left_grad = acc[0:node_count, cols]
                left_hess = acc[node_count : 2 * node_count, cols]
                if total_grad is None:
                    total_grad = jnp.broadcast_to(left_grad[:, BINS - 1 : BINS], left_grad.shape)
                    total_hess = jnp.broadcast_to(left_hess[:, BINS - 1 : BINS], left_hess.shape)
                    base = total_grad * total_grad / (total_hess + l2_penalty)
                right_grad = total_grad - left_grad
                gain = 0.5 * (
                    left_grad * left_grad / (left_hess + l2_penalty)
                    + right_grad * right_grad / (total_hess - left_hess + l2_penalty)
                    - base
                )
                top = jnp.max(jnp.where(lane < BINS - 1, gain, -jnp.inf), axis=1, keepdims=True)
                tops = jnp.where(lane == piece * share + k, top, tops)
    turned = tops.T
    best_out[...] = turned[0:owned]
    best = jnp.max(turned[0:owned], axis=0, keepdims=True)
    top_snd[...] = best

    with jax.named_scope("top"):
        others = [(d, e) for d in (*issue, 0) for e in range(n_rep) if d or e]
        for i, (d, e) in enumerate(others):
            remote(top_snd, top_rcv.at[i], top_ss, top_rs, at(d, e)).start()
        tops_all = all_of(top_rcv, top_ss, top_rs)
        tops_all.wait_recv()
        for i in range(len(others)):
            best = jnp.maximum(best, top_rcv[i])
        node_best[...] = best
        for sent in (sides, tops_all, *map(early_of, range(len(groups))), *map(fan_of, range(len(groups)))):
            sent.wait_send()
        if pieces > 1:
            guesses.wait_send()
        if n_rows > 2:
            for i, (slots, rows) in enumerate(parts):
                all_of(bins_rcv.at[1 : n_rows - 1, slots, rows], bins_ss.at[i], bins_rs.at[0]).wait_send()
        for i in range(len(ends)):
            ended(i).wait_send()


def hand_on(*refs):
    for src, dst in zip(refs[:3], refs[3:]):
        dst[...] = src[...]


def body(n_rows, n_rep, binned, gradients, hessians, parents, split_feature, split_bin, elected):
    rows_here, block_width = binned.shape
    node_count, slots_here = elected.shape
    owned = slots_here // n_rows
    pieces = 2 if owned % 16 == 0 and rows_here > 2 * LANES else 1
    parts, steps = parts_of(pieces, owned, rows_here)
    parts, ends = len(parts), sum(map(len, steps))
    f32 = jnp.float32
    vmem = pl.BlockSpec(memory_space=pltpu.VMEM)
    dma = pltpu.SemaphoreType.DMA
    order = tuple(range(1, n_rows))
    args = (split_feature, split_bin, binned, gradients, hessians, parents.reshape(1, rows_here), elected)
    made = pl.pallas_call(
        functools.partial(kernel, n_rows, n_rep, pieces, order, order),
        out_shape=(
            jax.ShapeDtypeStruct((1, rows_here), jnp.int32),
            jax.ShapeDtypeStruct((owned, node_count), f32),
            jax.ShapeDtypeStruct((1, node_count), f32),
        ),
        in_specs=[pl.BlockSpec(memory_space=pltpu.HBM)] * 7,
        out_specs=(vmem, vmem, vmem),
        scratch_shapes=[
            pltpu.SMEM(split_feature.shape, jnp.int32),
            pltpu.SMEM(split_bin.shape, jnp.int32),
            pltpu.VMEM(binned.shape, jnp.int32),
            pltpu.VMEM(gradients.shape, gradients.dtype),
            pltpu.VMEM(hessians.shape, hessians.dtype),
            pltpu.VMEM((1, rows_here), jnp.int32),
            pltpu.VMEM(elected.shape, jnp.int32),
            pltpu.VMEM((slots_here, rows_here), jnp.int32),
            pltpu.VMEM((1, rows_here), f32),
            pltpu.VMEM((n_rep - 1, 1, rows_here), f32),
            pltpu.VMEM((n_rows, 2, owned // pieces, LANES), jnp.int32),
            pltpu.VMEM((n_rows, 2, owned // pieces, LANES), jnp.int32),
            pltpu.VMEM((n_rows, owned, rows_here), jnp.int32),
            pltpu.VMEM((n_rows, owned, rows_here), jnp.int32),
            pltpu.VMEM((n_rep, n_rows, n_rep + 3, 1, rows_here // n_rep), f32),
            pltpu.VMEM((2, rows_here), f32),
            pltpu.VMEM((n_rows, 2 * node_count, rows_here), jnp.bfloat16),
            pltpu.VMEM((owned * BINS, rows_here), jnp.float8_e4m3fn),
            pltpu.VMEM((2 * node_count, owned * BINS), f32),
            pltpu.VMEM((1, node_count), f32),
            pltpu.VMEM((n_rows * n_rep - 1, 1, node_count), f32),
            dma((7,)),
        ]
        + [dma(())] * 2
        + [dma((1,))] * 4
        + [dma(())] * 2
        + [dma((parts + ends,)), dma(((n_rows - 2) * parts + ends,))]
        + [dma(())] * 2,
        compiler_params=pltpu.CompilerParams(collective_id=0, has_side_effects=True, vmem_limit_bytes=16 * 2**20),
    )(*(pltpu.with_memory_space_constraint(a, pltpu.HBM) for a in args))
    new_nodes, best, node_best = pl.pallas_call(
        hand_on,
        out_shape=tuple(jax.ShapeDtypeStruct(a.shape, a.dtype) for a in made),
        in_specs=[vmem] * 3,
        out_specs=(vmem,) * 3,
        compiler_params=pltpu.CompilerParams(vmem_limit_bytes=2**20),
    )(*made)
    return (
        new_nodes.reshape(rows_here),
        best.T.reshape(node_count, 1, owned),
        node_best.reshape(node_count),
    )


def solution(mesh):
    return jax.shard_map(
        functools.partial(body, mesh.shape["rows"], mesh.shape["rep"]),
        mesh=mesh,
        in_specs=(P("rows", "rep"), P("rows"), P("rows"), P("rows"), P(), P(), P(None, "rep")),
        out_specs=(P("rows"), P(None, "rep", "rows"), P()),
        check_vma=False,
    )
```

time: 28.7 us -> 27.9 us (0.972)
  Pallas kernels: 27.9 us -> 27.1 us
    pallas_call x1, Pallas kernels: 27.3 us -> 26.5 us  [body(): pl.pallas_call(functools.partial(kernel, n_rows, n_rep, pieces, order, or...]
where the time goes in v3:
time: 27.9 us; the launch traced here: 27.8 us
  Pallas kernels  27.1 us (97%)
  between operations  0.64 us (2%)
    pallas_call x1, Pallas kernels, body(): pl.pallas_call(functools.partial(kernel, n_rows, n_rep, pieces, order, or...  26.5 us
    pallas_call x1, Pallas kernels, body(): pl.pallas_call(hand_on, out_shape=tuple((jax.ShapeDtypeStruct(a.shape, a....  0.6 us

profile of v3, /device:TPU:0, one launch (start us, length us, event | category | flops | bytes accessed | tf_op | source)
XLA Modules:
  0.0 27.8 jit_solution(1172921271971686737)
XLA Ops:
  0.6 26.5 %shard_map.94 = (s32[1,1024]{1,0:T(1,128)S(1)}, f32[16,32]{1,0:T(8,128)S(1)}, f32[1,32]{1,0:T(1,128)S(1)}) custom-call(s32[16]{0:T(128)} %split_feature_in.1, s32[16]{0:T(128)} %split_bin_in.1, s32[1024,256]{1,0:T(8,128)} %binned_in.1, bf16[1024]{0:T(1024)(128)(2,1)} %gradients_in.1, bf16[1024]{0:T(1024)(128)(2,1)} %hessians_in.1, s32[1,1024]{1,0:T(1,128)} %bitcast.6, ...), custom_call_target="tpu_custom_call" | custom-call | tf_op jit(solution)/shard_map/pallas_call | solution.py:363
  27.2 0.6 %shard_map.95 = (s32[1,1024]{1,0:T(1,128)}, f32[16,32]{1,0:T(8,128)}, f32[1,32]{1,0:T(1,128)}) custom-call(s32[1,1024]{1,0:T(1,128)S(1)} %get-tuple-element.9.refs_0_, f32[16,32]{1,0:T(8,128)S(1)} %get-tuple-element.10.refs_1_, f32[1,32]{1,0:T(1,128)S(1)} %get-tuple-element.11.refs_2_), custom_call_target="tpu_custom_call" | custom-call | tf_op jit(solution)/shard_map/pallas_call | solution.py:403

commit v4 on v3

--- a/solution.py
+++ b/solution.py
@@ -174,7 +174,7 @@
                 two = both_bins[j * owned + owned - share : (j + 1) * owned, 0:LANES]
                 guess_snd[j, 0] = two & 255
                 guess_snd[j, 1] = lax.shift_right_logical(two, 8)
-            for d in issue:
+            for d in issue[::-1]:
                 remote(
                     guess_snd.at[partner_of(n_rows, me, d)], guess_rcv.at[slot_of[d]], guess_ss, guess_rs, at(d, 0)
                 ).start()

time: 27.9 us -> 27.8 us (level)
  no operation moved by 1% of the time
where the time goes in v4:
time: 27.8 us; the launch traced here: 27.6 us
  Pallas kernels  27 us (97%)
  between operations  0.64 us (2%)
    pallas_call x1, Pallas kernels, body(): pl.pallas_call(functools.partial(kernel, n_rows, n_rep, pieces, order, or...  26.4 us
    pallas_call x1, Pallas kernels, body(): pl.pallas_call(hand_on, out_shape=tuple((jax.ShapeDtypeStruct(a.shape, a....  0.6 us

profile of v4, /device:TPU:0, one launch (start us, length us, event | category | flops | bytes accessed | tf_op | source)
XLA Modules:
  0.0 27.6 jit_solution(10792900193994980968)
XLA Ops:
  0.6 26.4 %shard_map.94 = (s32[1,1024]{1,0:T(1,128)S(1)}, f32[16,32]{1,0:T(8,128)S(1)}, f32[1,32]{1,0:T(1,128)S(1)}) custom-call(s32[16]{0:T(128)} %split_feature_in.1, s32[16]{0:T(128)} %split_bin_in.1, s32[1024,256]{1,0:T(8,128)} %binned_in.1, bf16[1024]{0:T(1024)(128)(2,1)} %gradients_in.1, bf16[1024]{0:T(1024)(128)(2,1)} %hessians_in.1, s32[1,1024]{1,0:T(1,128)} %bitcast.6, ...), custom_call_target="tpu_custom_call" | custom-call | tf_op jit(solution)/shard_map/pallas_call | solution.py:363
  27.0 0.6 %shard_map.95 = (s32[1,1024]{1,0:T(1,128)}, f32[16,32]{1,0:T(8,128)}, f32[1,32]{1,0:T(1,128)}) custom-call(s32[1,1024]{1,0:T(1,128)S(1)} %get-tuple-element.9.refs_0_, f32[16,32]{1,0:T(8,128)S(1)} %get-tuple-element.10.refs_1_, f32[1,32]{1,0:T(1,128)S(1)} %get-tuple-element.11.refs_2_), custom_call_target="tpu_custom_call" | custom-call | tf_op jit(solution)/shard_map/pallas_call | solution.py:403
